TPU v7x, 32 devices: a whole 2x2x4 slice. The times are simulated.
32 devices in a mesh: section: 4 (over y, core), seq: 8 (over z, x).
Axes of the slice: x: 2, y: 2, z: 4, core: 2. Of those that a mesh axis runs over, the one named last changes fastest.
Arguments:
- queries: bfloat16 [4, 64, 4096], P('section', 'seq'), may hold values from -110 to 110
- key_value_pages: bfloat16 [4, 16, 4, 2048], P('section', 'seq'), may hold values from -5 to 5
- block_table: int32 [4, 16], replicated, may hold values from 0 to 15, as said below
- page_mask: int32 [4, 64], replicated, may hold values from 0 to 1, as said below
- noise_level: int32 [4], replicated, may hold values from 0 to 15
- level_gate: float32 [16, 4096], replicated, may hold values from 0.5 to 1.5
Outputs:
- attended: bfloat16 [4, 64, 4096], P('section', 'seq')
Inputs may be any that keep to these rules, and one draw needn't show every extreme that they name: `block_table`: each row is a permutation of 0 to 15. `page_mask`: a query span sees all pages of its own span, none of later spans, and some pages of earlier spans.
All inputs are finite; a program needn't handle non-finite values.
Results may differ from a plain program's by a relative error of at most 0.0065.
Values may be sent and summed in bfloat16 or wider, within the bound.
No kernel may reach another device: no remote copies, remote signals or barrier semaphores. Data moves between devices by JAX's collectives and lax.ppermute only.
A program may use at most 64 MiB of HBM per device.

v0:
```python
import jax
import jax.numpy as jnp
from jax import lax
from jax.sharding import PartitionSpec as P

QUERY_HEADS = 32
KEY_VALUE_HEADS = 8
HEAD_WIDTH = 128
eps = 1e-06


def body(queries, key_value_pages, block_table, page_mask, noise_level, level_gate):
    seq_count = lax.axis_size("seq")
    section_index = lax.axis_index("section")
    seq_index = lax.axis_index("seq")
    spans = page_mask.shape[0]
    pages = block_table.shape[1]
    page_length = key_value_pages.shape[2]
    span_group = QUERY_HEADS // KEY_VALUE_HEADS
    per_device = QUERY_HEADS // seq_count
    length = queries.shape[1] * seq_count
    scale = HEAD_WIDTH ** (-0.5)
    headed_queries = lax.all_to_all(queries, "seq", split_axis=2, concat_axis=1, tiled=True)
    query_rows = headed_queries.reshape(length, per_device, HEAD_WIDTH)
    onehot = (block_table[:, :, None] == jnp.arange(pages, dtype=jnp.int32)[None, None, :]).astype(
        jnp.float32
    )
    mask_row = lax.dynamic_index_in_dim(page_mask, section_index, 0, keepdims=False).reshape(
        spans, pages
    )
    visible = jnp.einsum("ci,cip->cp", mask_row.astype(jnp.float32), onehot)
    token_visible = jnp.repeat(visible, page_length, axis=1) > 0.5
    level_row = (
        jnp.arange(level_gate.shape[0], dtype=jnp.int32) == noise_level[section_index]
    ).astype(jnp.float32)
    gate_full = jnp.dot(level_row[None, :], level_gate, precision=lax.Precision.HIGHEST)[0].reshape(
        QUERY_HEADS, HEAD_WIDTH
    )
    gate_own = lax.dynamic_slice_in_dim(gate_full, seq_index * per_device, per_device, 0)

    def attend(carry, block, span):
        running, total, accum = carry
        keys = block[:, :, 0, :].reshape(length, per_device, HEAD_WIDTH)
        value_rows = block[:, :, 1, :].reshape(length, per_device, HEAD_WIDTH)
        seen = lax.dynamic_index_in_dim(token_visible, span, 0, keepdims=False)
        scores = (
            jnp.einsum("qhd,khd->qhk", query_rows, keys, preferred_element_type=jnp.float32) * scale
        )
        scores = jnp.where(seen[None, None, :], scores, -1e30)
        newmax = jnp.maximum(running, jnp.max(scores, axis=-1))
        shrink = jnp.exp(running - newmax)
        weights = jnp.where(seen[None, None, :], jnp.exp(scores - newmax[:, :, None]), 0.0)
        total = total * shrink + jnp.sum(weights, axis=-1)
        update = jnp.einsum(
            "qhk,khd->qhd",
            weights.astype(jnp.bfloat16),
            value_rows,
            preferred_element_type=jnp.float32,
        )
        accum = accum * shrink[:, :, None] + update
        return (newmax, total, accum)

    def visit(carry, block, span):
        return attend(carry, block, span)

    initial = (
        jnp.full((length, per_device), -1e30, jnp.float32),
        jnp.zeros((length, per_device), jnp.float32),
        jnp.zeros((length, per_device, HEAD_WIDTH), jnp.float32),
    )
    span_count = key_value_pages.shape[0]
    local_span_count = key_value_pages.shape[1]
    group_spread = key_value_pages.reshape(
        span_count, local_span_count, page_length, 2, KEY_VALUE_HEADS, 1, HEAD_WIDTH
    )
    group_spread = jnp.broadcast_to(
        group_spread,
        (span_count, local_span_count, page_length, 2, KEY_VALUE_HEADS, span_group, HEAD_WIDTH),
    )
    mine = lax.all_to_all(
        group_spread.reshape(
            span_count, local_span_count, page_length, 2, QUERY_HEADS * HEAD_WIDTH
        ),
        "seq",
        split_axis=4,
        concat_axis=1,
        tiled=True,
    )
    piece = lax.all_gather(mine, "section", axis=0, tiled=True)

    def inner(offset, state):
        block = lax.dynamic_index_in_dim(piece, offset, 0, keepdims=False)
        return visit(state, block, offset)

    carry = lax.fori_loop(0, piece.shape[0], inner, initial)
    running, total, accum = carry
    mixed = accum / total[:, :, None]
    normed = mixed * lax.rsqrt(jnp.mean(mixed * mixed, axis=-1, keepdims=True) + eps)
    gated = (
        (normed * gate_own[None, :, :])
        .astype(jnp.bfloat16)
        .reshape(1, length, per_device * HEAD_WIDTH)
    )
    return lax.all_to_all(gated, "seq", split_axis=1, concat_axis=2, tiled=True)


def solution(mesh):
    return jax.shard_map(
        body,
        mesh=mesh,
        in_specs=(P("section", "seq", None), P("section", "seq", None, None), P(), P(), P(), P()),
        out_specs=P("section", "seq", None),
        check_vma=False,
    )
```

profile of v0, /device:TPU:0, one launch (start us, length us, event | category | flops | bytes accessed | tf_op | source)
XLA Modules:
  0.0 108.3 jit_solution(8707232071351404596)
XLA Ops:
  0.0 4.3 %copy.54 = bf16[1,8,4096]{1,0,2:T(2,128)(2,1)S(1)} copy(bf16[1,8,4096]{2,1,0:T(8,128)(2,1)} %param.8) | data formatting | bytes 131072 | tf_op args[0]
  4.3 0.5 broadcast.64
  4.8 22.4 %reduce.4 = bf16[4096,8]{1,0:T(8,128)(2,1)S(1)} reduce(bf16[4096,1,8]{2,1,0:T(2,128)(2,1)S(1)} %bitcast.71, bf16[]{:T(256)} %broadcast.64), dimensions={1}, to_apply=%bitcast.48.reduce_sub_computation | reduce | bytes 131074
  27.2 1.7 %reshape.58 = bf16[8,2,2048]{2,1,0:T(2,128)(2,1)} reshape(bf16[4096,8]{1,0:T(8,128)(2,1)S(1)} %reduce.4) | data formatting | bytes 131072
  28.9 7.3 %all-to-all-start.1 = ((bf16[8,2,2048]{2,1,0:T(2,128)(2,1)}), bf16[8,2,2048]{2,1,0:T(2,128)(2,1)S(1)}, u32[]{:S(2)}, u32[]{:S(2)}) async-start(bf16[8,2,2048]{2,1,0:T(2,128)(2,1)} %reshape.58), calls=%async_computation.1 | async-start | bytes 131072 | tf_op jit(solution)/shard_map/all_to_all | solution.py:23
  36.2 0.7 convert_reduce_fusion
  37.0 0.2 fusion.16
  37.5 1.3 %copy.50 = bf16[2,4,2,8,128]{1,2,0,4,3:T(2,128)(2,1)S(1)} copy(bf16[2,4,2,8,128]{4,3,2,1,0:T(8,128)(2,1)S(1)} %broadcast_in_dim.81) | data formatting | bytes 65536 | tf_op jit(solution)/shard_map/broadcast_in_dim | solution.py:76
  38.8 5.8 %broadcast_in_dim.82 = bf16[2,4,2,8,4,128]{1,2,0,5,4,3:T(2,128)(2,1)} broadcast(bf16[2,4,2,8,128]{1,2,0,4,3:T(2,128)(2,1)S(1)} %copy.50), dimensions={0,1,2,3,5} | broadcast | bytes 163840 | tf_op jit(solution)/shard_map/broadcast_in_dim | solution.py:76
  44.6 9.3 %reshape.56 = bf16[8,2,4096]{2,1,0:T(2,128)(2,1)} reshape(bf16[4096,1,2,2,4]{4,3,2,1,0:T(2,128)(2,1)} %bitcast.68) | data formatting | bytes 262144
  53.9 0.7 dynamic_slice.27
  54.6 6.0 %all-to-all-start = ((bf16[8,2,4096]{2,1,0:T(2,128)(2,1)}), bf16[8,2,4096]{2,1,0:T(2,128)(2,1)S(1)}, u32[]{:S(2)}, u32[]{:S(2)}) async-start(bf16[8,2,4096]{2,1,0:T(2,128)(2,1)} %reshape.56), calls=%async_computation | async-start | bytes 262144 | tf_op jit(solution)/shard_map/all_to_all | solution.py:80
  60.6 0.9 fusion.13
  61.5 2.8 %reshape.59 = bf16[4096,1,8]{2,1,0:T(2,128)(2,1)S(1)} reshape(bf16[8,2,2048]{2,1,0:T(2,128)(2,1)S(1)} %all-to-all-done.1) | data formatting | bytes 131072
  64.3 1.9 %copy.55 = bf16[1,8,4096]{2,1,0:T(8,128)(2,1)S(1)} copy(bf16[1,8,4096]{1,0,2:T(2,128)(2,1)S(1)} %bitcast.72) | data formatting | bytes 131072 | tf_op jit(solution)/shard_map/all_to_all | solution.py:23
  66.3 1.6 %all-to-all-done = bf16[8,2,4096]{2,1,0:T(2,128)(2,1)S(1)} async-done(((bf16[8,2,4096]{2,1,0:T(2,128)(2,1)}), bf16[8,2,4096]{2,1,0:T(2,128)(2,1)S(1)}, u32[]{:S(2)}, u32[]{:S(2)}) %all-to-all-start) | async-done | bytes 131104 | tf_op jit(solution)/shard_map/all_to_all | solution.py:80
  67.9 10.0 %reshape.57 = bf16[4096,1,2,2,4]{4,3,2,1,0:T(2,128)(2,1)} reshape(bf16[8,2,4096]{2,1,0:T(2,128)(2,1)S(1)} %all-to-all-done) | data formatting | bytes 262144
  77.9 6.1 %copy.66 = bf16[1,2,4,2,8,512]{5,4,3,2,1,0:T(8,128)(2,1)S(1)} copy(bf16[1,2,4,2,8,512]{2,3,1,5,4,0:T(2,128)(2,1)} %bitcast.69) | data formatting | bytes 262144 | tf_op jit(solution)/shard_map/all_to_all | solution.py:80
  84.2 7.2 %all_gather.3 = bf16[4,16,4,2,512]{4,1,3,2,0:T(8,128)(2,1)S(1)} all-gather(bf16[1,16,4,2,512]{4,1,3,2,0:T(8,128)(2,1)S(1)} %copy.53), channel_id=1, replica_groups=mesh['section'=4,'seq'=8] {'section'}, dimensions={0}, use_global_device_ids=true | all-gather | bytes 655360 | tf_op jit(solution)/shard_map/all_gather | solution.py:89
  91.4 3.6 %while.18 = (s32[]{:T(128)}, f32[64,4]{0,1:T(4,128)S(1)}, f32[64,4]{0,1:T(4,128)S(1)}, f32[64,4,128]{2,0,1:T(8,128)S(1)}, pred[4,64]{1,0:T(4,128)(4,1)S(1)}, /*i...) while((s32[]{:T(128)}, f32[64,4]{0,1:T(4,128)S(1)}, ...), condition=%wide.region_3.4_spmd.clone, body=%wide.region_0.3_spmd.clone.sunk | while | flops 8635651 | bytes 1720753 | solution.py:95
  91.6 0.2 fusion.39
  92.0 0.3 fusion.42
  92.6 0.2 fusion.39
  92.9 0.3 fusion.42
  93.5 0.2 fusion.39
  93.8 0.3 fusion.42
  94.4 0.2 fusion.39
  94.8 0.3 fusion.42
  95.1 0.2 multiply_reduce_fusion
  95.5 1.0 reduce.5
  96.5 11.1 %all_to_all.51 = bf16[8,2,2048]{2,1,0:T(2,128)(2,1)S(1)} all-to-all(bf16[8,2,2048]{2,1,0:T(2,128)(2,1)S(1)} %reshape.60), channel_id=1, replica_groups=mesh['section'=4,'seq'=8] {'seq'}, dimensions={0} | all-to-all | bytes 131072 | tf_op jit(solution)/shard_map/all_to_all | solution.py:104
  107.7 0.6 copy.68
  (70 shorter events, 2.4 us)
Async XLA Ops:
  0.0 60.6 %copy-start = (f32[16,4096]{1,0:T(8,128)S(1)}, f32[16,4096]{1,0:T(8,128)}, u32[]{:S(2)}) copy-start(f32[16,4096]{1,0:T(8,128)} %param.13) | copy-start | bytes 786436
  0.0 37.0 %copy-start.2 = (s32[4,16]{1,0:T(4,128)S(1)}, s32[4,16]{1,0:T(4,128)}, u32[]{:S(2)}) copy-start(s32[4,16]{1,0:T(4,128)} %param.10) | copy-start | bytes 772
  0.0 37.4 %copy-start.1 = (bf16[1,2,4,2048]{3,2,1,0:T(4,128)(2,1)S(1)}, bf16[1,2,4,2048]{3,2,1,0:T(4,128)(2,1)}, u32[]{:S(2)}) copy-start(bf16[1,2,4,2048]{3,2,1,0:T(4,128)(2,1)} %param.9) | copy-start | bytes 98308
  28.9 25.7 %all-to-all-start.1 = ((bf16[8,2,2048]{2,1,0:T(2,128)(2,1)}), bf16[8,2,2048]{2,1,0:T(2,128)(2,1)S(1)}, u32[]{:S(2)}, u32[]{:S(2)}) async-start(bf16[8,2,2048]{2,1,0:T(2,128)(2,1)} %reshape.58), calls=%async_computation.1 | async-start | bytes 131072 | tf_op jit(solution)/shard_map/all_to_all | solution.py:23
  38.8 15.2 %copy-start.3 = (s32[4]{0:T(128)S(1)}, s32[4]{0:T(128)}, u32[]{:S(2)}) copy-start(s32[4]{0:T(128)} %param.12) | copy-start | bytes 52
  54.6 13.3 %all-to-all-start = ((bf16[8,2,4096]{2,1,0:T(2,128)(2,1)}), bf16[8,2,4096]{2,1,0:T(2,128)(2,1)S(1)}, u32[]{:S(2)}, u32[]{:S(2)}) async-start(bf16[8,2,4096]{2,1,0:T(2,128)(2,1)} %reshape.56), calls=%async_computation | async-start | bytes 262144 | tf_op jit(solution)/shard_map/all_to_all | solution.py:80
where the time goes:
time: 109 us; the launch traced here: 108 us
  local copies, waits for them, and re-layouts  46.8 us (43%)
  other arithmetic  24.9 us (23%)
  blocking collectives  18.3 us (17%)
  starting transfers between devices  13.3 us (12%)
  matrix products  2.95 us (3%)
  waiting for transfers between devices  1.64 us (2%)
    unnamed x19, local copies, waits for them, and re-layouts  29.4 us
    unnamed x5, other arithmetic  23.3 us
    all_to_all x1, blocking collectives, body(): return lax.all_to_all(gated, 'seq', split_axis=1, concat_axis=2, tiled=True)  11.1 us
    all_to_all x1, starting transfers between devices, body(): lax.all_to_all(queries, 'seq', split_axis=2, concat_axis=1, tiled=True)  7.29 us
    all_gather x1, blocking collectives, body(): piece = lax.all_gather(mine, 'section', axis=0, tiled=True)  7.2 us
    broadcast_in_dim x3, local copies, waits for them, and re-layouts, body(): jnp.broadcast_to(group_spread, (span_count, local_span_count, page_length...  7.15 us
    all_to_all x3, local copies, waits for them, and re-layouts, body(): lax.all_to_all(group_spread.reshape(span_count, local_span_count, page_le...  6.26 us
    all_to_all x1, starting transfers between devices, body(): lax.all_to_all(group_spread.reshape(span_count, local_span_count, page_le...  5.98 us
  transfers between devices with their start and end apart: 2, of which 1 were waited for; matrix products, arithmetic and copies ran while one was open for 22% of the time, Pallas kernels for 0%

commit v1 on v0

--- a/solution.py
+++ b/solution.py
@@ -77,14 +77,22 @@
         group_spread,
         (span_count, local_span_count, page_length, 2, KEY_VALUE_HEADS, span_group, HEAD_WIDTH),
     )
-    mine = lax.all_to_all(
-        group_spread.reshape(
-            span_count, local_span_count, page_length, 2, QUERY_HEADS * HEAD_WIDTH
+    mine = jnp.concatenate(
+        lax.all_to_all(
+            jnp.stack(
+                jnp.split(
+                    group_spread.reshape(
+                        span_count, local_span_count, page_length, 2, QUERY_HEADS * HEAD_WIDTH
+                    ),
+                    lax.axis_size("seq"),
+                    axis=4,
+                )
+            ),
+            "seq",
+            0,
+            0,
         ),
-        "seq",
-        split_axis=4,
-        concat_axis=1,
-        tiled=True,
+        axis=1,
     )
     piece = lax.all_gather(mine, "section", axis=0, tiled=True)
 

time: 109 us -> 81 us (0.74)
  local copies, waits for them, and re-layouts: 46.8 us -> 19.1 us
    unnamed x19 -> x24, local copies, waits for them, and re-layouts: 29.4 us -> 14.3 us
    broadcast_in_dim x3 -> x4, local copies, waits for them, and re-layouts: 7.15 us -> 0.11 us  [body(): jnp.broadcast_to(group_spread, (span_count, local_span_count, page_length...]
    all_to_all x3 -> x1, local copies, waits for them, and re-layouts: 6.26 us -> 0.11 us  [body(): lax.all_to_all(jnp.stack(jnp.split(group_spread.reshape(span_count, local...]
  transfers between devices with their start and end apart: 2 -> 2, of which waited for: 1 -> 2; matrix products, arithmetic and copies ran while one was open for 22% -> 15% of each run, Pallas kernels for 0% -> 0%
where the time goes in v1:
time: 81 us; the launch traced here: 80.5 us
  other arithmetic  24.8 us (31%)
  local copies, waits for them, and re-layouts  19.1 us (24%)
  blocking collectives  18.2 us (22%)
  starting transfers between devices  13.2 us (16%)
  matrix products  2.89 us (4%)
  waiting for transfers between devices  1.78 us (2%)
    unnamed x5, other arithmetic  23.3 us
    unnamed x24, local copies, waits for them, and re-layouts  14.3 us
    all_to_all x1, blocking collectives, body(): return lax.all_to_all(gated, 'seq', split_axis=1, concat_axis=2, tiled=True)  11 us
    all_to_all x1, starting transfers between devices, body(): lax.all_to_all(queries, 'seq', split_axis=2, concat_axis=1, tiled=True)  7.28 us
    all_gather x1, blocking collectives, body(): piece = lax.all_gather(mine, 'section', axis=0, tiled=True)  7.2 us
    all_to_all x1, starting transfers between devices, body(): lax.all_to_all(jnp.stack(jnp.split(group_spread.reshape(span_count, local...  5.91 us
    all_to_all x2, local copies, waits for them, and re-layouts, body(): lax.all_to_all(queries, 'seq', split_axis=2, concat_axis=1, tiled=True)  1.9 us
    all_to_all x1, waiting for transfers between devices, body(): lax.all_to_all(jnp.stack(jnp.split(group_spread.reshape(span_count, local...  1.7 us
  transfers between devices with their start and end apart: 2, of which 2 were waited for; matrix products, arithmetic and copies ran while one was open for 15% of the time, Pallas kernels for 0%

profile of v1, /device:TPU:0, one launch (start us, length us, event | category | flops | bytes accessed | tf_op | source)
XLA Modules:
  0.0 80.5 jit_solution(179733552045157433)
XLA Ops:
  0.0 4.3 %copy.44 = bf16[1,8,4096]{1,0,2:T(2,128)(2,1)S(1)} copy(bf16[1,8,4096]{2,1,0:T(8,128)(2,1)} %param.8) | data formatting | bytes 131072 | tf_op args[0]
  4.3 0.5 broadcast.64
  4.8 22.3 %reduce.4 = bf16[4096,8]{1,0:T(8,128)(2,1)S(1)} reduce(bf16[4096,1,8]{2,1,0:T(2,128)(2,1)S(1)} %bitcast.98, bf16[]{:T(256)} %broadcast.64), dimensions={1}, to_apply=%bitcast.77.reduce_sub_computation | reduce | bytes 131074
  27.2 1.7 %reshape.60 = bf16[8,2,2048]{2,1,0:T(2,128)(2,1)} reshape(bf16[4096,8]{1,0:T(8,128)(2,1)S(1)} %reduce.4) | data formatting | bytes 131072
  28.9 7.3 %all-to-all-start.1 = ((bf16[8,2,2048]{2,1,0:T(2,128)(2,1)}), bf16[8,2,2048]{2,1,0:T(2,128)(2,1)S(1)}, u32[]{:S(2)}, u32[]{:S(2)}) async-start(bf16[8,2,2048]{2,1,0:T(2,128)(2,1)} %reshape.60), calls=%async_computation.1 | async-start | bytes 131072 | tf_op jit(solution)/shard_map/all_to_all | solution.py:23
  36.3 0.6 constant_dynamic-update-slice_fusion.7
  36.9 0.6 constant_dynamic-update-slice_fusion.6
  37.5 0.6 constant_dynamic-update-slice_fusion.5
  38.1 0.6 constant_dynamic-update-slice_fusion.4
  38.7 0.6 constant_dynamic-update-slice_fusion.3
  39.3 0.6 constant_dynamic-update-slice_fusion.2
  39.9 0.6 constant_dynamic-update-slice_fusion.1
  40.5 0.7 convert_reduce_fusion
  41.3 0.2 fusion.16
  41.7 0.6 dynamic_slice.27
  42.4 0.6 constant_dynamic-update-slice_fusion
  43.0 5.9 %all-to-all-start = ((bf16[8,1,2,4,2,512]{5,3,2,4,1,0:T(4,128)(2,1)}), bf16[8,1,2,4,2,512]{5,3,2,4,1,0:T(4,128)(2,1)S(1)}, u32[]{:S(2)}, u32[]{:S(2)}) async-start(bf16[8,1,2,4,2,512]{5,3,2,4,1,0:T(4,128)(2,1)} %constant_dynamic-update-slice_fusion), calls=%async_computation | async-start | bytes 262144 | tf_op jit(solution)/shard_map/all_to_all | solution.py:81
  49.0 0.8 %fusion.13 = f32[1,32,128]{2,0,1:T(1,128)S(1)} fusion(s32[]{:T(128)} %bitcast.13, f32[16,4096]{1,0:T(8,128)S(1)} %copy-done), kind=kOutput, calls=%fused_computation.22 | convolution fusion | flops 786448 | bytes 278532 | tf_op jit(solution)/shard_map/dot_general | solution.py:36
  49.8 2.8 %reshape.61 = bf16[4096,1,8]{2,1,0:T(2,128)(2,1)S(1)} reshape(bf16[8,2,2048]{2,1,0:T(2,128)(2,1)S(1)} %all-to-all-done.1) | data formatting | bytes 131072
  52.6 1.9 %copy.45 = bf16[1,8,4096]{2,1,0:T(8,128)(2,1)S(1)} copy(bf16[1,8,4096]{1,0,2:T(2,128)(2,1)S(1)} %bitcast.99) | data formatting | bytes 131072 | tf_op jit(solution)/shard_map/all_to_all | solution.py:23
  54.6 1.7 %all-to-all-done = bf16[8,1,2,4,2,512]{5,3,2,4,1,0:T(4,128)(2,1)S(1)} async-done(((bf16[8,1,2,4,2,512]{5,3,2,4,1,0:T(4,128)(2,1)}), bf16[8,1,2,4,2,512]{5,3,2,4,1,0:T(4,128)(2,1)S(1)}, u32[]{:S(2)}, u32[]{:S(2)}) %all-to-all-start) | async-done | bytes 131104 | tf_op jit(solution)/shard_map/all_to_all | solution.py:81
  56.5 7.2 %all_gather.3 = bf16[4,16,4,2,512]{4,1,3,2,0:T(8,128)(2,1)S(1)} all-gather(bf16[1,16,4,2,512]{4,1,3,2,0:T(8,128)(2,1)S(1)} %copy.43), channel_id=1, replica_groups=mesh['section'=4,'seq'=8] {'section'}, dimensions={0}, use_global_device_ids=true | all-gather | bytes 655360 | tf_op jit(solution)/shard_map/all_gather | solution.py:97
  63.7 3.7 %while.18 = (s32[]{:T(128)}, f32[64,4]{0,1:T(4,128)S(1)}, f32[64,4]{0,1:T(4,128)S(1)}, f32[64,4,128]{2,0,1:T(8,128)S(1)}, pred[4,64]{1,0:T(4,128)(4,1)S(1)}, /*i...) while((s32[]{:T(128)}, f32[64,4]{0,1:T(4,128)S(1)}, ...), condition=%wide.region_3.4_spmd.clone, body=%wide.region_0.3_spmd.clone.sunk | while | flops 8635651 | bytes 1720753 | solution.py:103
  63.9 0.2 fusion.39
  64.2 0.3 fusion.42
  65.2 0.3 fusion.42
  66.1 0.3 fusion.42
  67.0 0.3 fusion.42
  67.3 0.2 multiply_reduce_fusion
  67.8 0.9 %reduce.5 = bf16[64,512]{1,0:T(8,128)(2,1)S(1)} reduce(bf16[64,1,512]{2,1,0:T(2,128)(2,1)S(1)} %bitcast.100, bf16[]{:T(256)} %broadcast.64), dimensions={1}, to_apply=%bitcast.79.reduce_sub_computation | reduce | bytes 131074
  68.7 11.0 %all_to_all.38 = bf16[8,2,2048]{2,1,0:T(2,128)(2,1)S(1)} all-to-all(bf16[8,2,2048]{2,1,0:T(2,128)(2,1)S(1)} %reshape.62), channel_id=1, replica_groups=mesh['section'=4,'seq'=8] {'seq'}, dimensions={0} | all-to-all | bytes 131072 | tf_op jit(solution)/shard_map/all_to_all | solution.py:112
  79.8 0.6 copy.57
  (76 shorter events, 3.1 us)
Async XLA Ops:
  0.0 49.0 %copy-start = (f32[16,4096]{1,0:T(8,128)S(1)}, f32[16,4096]{1,0:T(8,128)}, u32[]{:S(2)}) copy-start(f32[16,4096]{1,0:T(8,128)} %param.13) | copy-start | bytes 786436
  4.8 31.3 %copy-start.1 = (bf16[1,2,4,2048]{3,2,1,0:T(4,128)(2,1)S(1)}, bf16[1,2,4,2048]{3,2,1,0:T(4,128)(2,1)}, u32[]{:S(2)}) copy-start(bf16[1,2,4,2048]{3,2,1,0:T(4,128)(2,1)} %param.9) | copy-start | bytes 98308
  4.8 36.5 %copy-start.2 = (s32[4,16]{1,0:T(4,128)S(1)}, s32[4,16]{1,0:T(4,128)}, u32[]{:S(2)}) copy-start(s32[4,16]{1,0:T(4,128)} %param.10) | copy-start | bytes 772
  4.8 36.9 %copy-start.3 = (s32[4]{0:T(128)S(1)}, s32[4]{0:T(128)}, u32[]{:S(2)}) copy-start(s32[4]{0:T(128)} %param.12) | copy-start | bytes 52
  28.9 14.2 %all-to-all-start.1 = ((bf16[8,2,2048]{2,1,0:T(2,128)(2,1)}), bf16[8,2,2048]{2,1,0:T(2,128)(2,1)S(1)}, u32[]{:S(2)}, u32[]{:S(2)}) async-start(bf16[8,2,2048]{2,1,0:T(2,128)(2,1)} %reshape.60), calls=%async_computation.1 | async-start | bytes 131072 | tf_op jit(solution)/shard_map/all_to_all | solution.py:23
  43.0 13.3 %all-to-all-start = ((bf16[8,1,2,4,2,512]{5,3,2,4,1,0:T(4,128)(2,1)}), bf16[8,1,2,4,2,512]{5,3,2,4,1,0:T(4,128)(2,1)S(1)}, u32[]{:S(2)}, u32[]{:S(2)}) async-start(bf16[8,1,2,4,2,512]{5,3,2,4,1,0:T(4,128)(2,1)} %constant_dynamic-update-slice_fusion), calls=%async_computation | async-start | bytes 262144 | tf_op jit(solution)/shard_map/all_to_all | solution.py:81
